TPU v7x, 256 devices: a 8x8x2 block of a 8x8x16 slice. The times are simulated.
256 devices in a mesh: grp: 2 (over z), trn: 64 (over y, x), tst: 2 (over core).
Axes of the slice: x: 8, y: 8, z: 2, core: 2. Of those that a mesh axis runs over, the one named last changes fastest.
The devices are a block of a 8x8x16 slice.
Arguments:
- test_points: bfloat16 [64, 8192], P(None, ('grp', 'tst')), parts along dimension 1, may hold values from -9 to 9
- train_points: bfloat16 [64, 524288], P(None, ('grp', 'trn')), parts along dimension 1, may hold values from -6 to 6
- weights: bfloat16 [524288], P(('grp', 'trn')), parts along dimension 0, may hold values from -6 to 6
- factor: bfloat16 [524288, 512], P(('grp', 'trn')), parts along dimension 0, may hold values from -1.14904852 to 1.14904852
Outputs:
- mean: float32 [8192], P(('grp', 'tst')), parts along dimension 0
- variance: float32 [8192], P(('grp', 'tst')), parts along dimension 0
There are 2 independent parts, one for each index of `grp`. A program takes and returns all parts, laid end to end along the dimension named above; each array names one. Nothing has to cross between parts.
All inputs are finite; a program needn't handle non-finite values.
Results may differ from a plain program's by a relative error of at most 0.0033.
Values sent between devices are 32-bit elements; how exact they have to be, the bound alone decides.
A program may use at most 64 MiB of HBM per device.

v0:
```python
import math
import jax
import jax.numpy as jnp
from jax import lax
from jax.sharding import Mesh
from jax.sharding import PartitionSpec as P

TRN = ("trn_0", "trn_1")
GRP_TRN = ("grp", "trn_0", "trn_1")


def scatter_axes(shard, axes, dim):
    if not axes:
        return shard
    nearer = lax.psum_scatter(shard, axes[0], scatter_dimension=dim, tiled=True)
    return scatter_axes(nearer, axes[1:], dim)


def turned_gather(arrays, axis, dims):
    turned = [jnp.moveaxis(a, dim, 0) for a, dim in zip(arrays, dims)]
    both = jnp.concatenate([t.reshape(len(t), -1) for t in turned], axis=1)
    result, at, outs = (lax.all_gather(both, axis, axis=0, tiled=True), 0, [])
    for t, dim in zip(turned, dims):
        piece = result[:, at : at + t[0].size].reshape(-1, *t.shape[1:])
        outs.append(jnp.moveaxis(piece, 0, dim))
        at += t[0].size
    return tuple(outs)


def on_device(test_points, train_points, weights, factor):
    rows = test_points.shape[1]
    local = train_points.shape[1]
    dim = test_points.shape[0]
    width = factor.shape[1]
    test_sq = jnp.sum(test_points.astype(jnp.float32) ** 2, axis=0)
    block = math.gcd(local, 1024)
    turns = local // block

    def step(index, carry):
        mean_acc, proj_acc = carry
        start = (index * block).astype(jnp.int32)
        points = lax.dynamic_slice_in_dim(train_points, start, block, 1)
        wblock = lax.dynamic_slice_in_dim(weights, start, block, 0)
        fblock = lax.dynamic_slice_in_dim(factor, start, block, 0)
        train_sq = jnp.sum(points.astype(jnp.float32) ** 2, axis=0)
        cross = lax.dot_general(
            test_points, points, (((0,), (0,)), ((), ())), preferred_element_type=jnp.float32
        )
        kernel = jnp.exp(
            -(test_sq[:, None] + train_sq[None, :] - 2.0 * cross) * (4.0 / dim)
        ).astype(jnp.bfloat16)
        mean_acc = mean_acc + jnp.dot(kernel, wblock, preferred_element_type=jnp.float32)
        proj_acc = proj_acc + jnp.dot(kernel, fblock, preferred_element_type=jnp.float32)
        return (mean_acc, proj_acc)

    init = (jnp.zeros((rows,), jnp.float32), jnp.zeros((rows, width), jnp.float32))
    mean_part, proj_part = lax.fori_loop(0, turns, step, init)
    mean_share, proj_share = (scatter_axes(mean_part, TRN, 0), scatter_axes(proj_part, TRN, 0))
    var_share = 1.0 - jnp.sum(proj_share * proj_share, axis=1)
    mean, variance = turned_gather((mean_share, var_share), TRN, (0, 0))
    return (mean, variance)


def solution(mesh):
    split = Mesh(
        mesh.devices.reshape(mesh.shape["grp"], 8, 8, mesh.shape["tst"]),
        ("grp", "trn_0", "trn_1", "tst"),
    )
    in_specs = (P(None, ("grp", "tst")), P(None, GRP_TRN), P(GRP_TRN), P(GRP_TRN, None))
    out_specs = (P(("grp", "tst")), P(("grp", "tst")))
    return jax.shard_map(
        on_device, mesh=split, in_specs=in_specs, out_specs=out_specs, check_vma=False
    )
```

profile of v0, /device:TPU:514, one launch (start us, length us, event | category | flops | bytes accessed | tf_op | source)
XLA Modules:
  0.0 241.4 jit_solution(6877016414136777848)
XLA Ops:
  7.3 1.0 multiply_reduce_fusion.1
  8.3 61.1 %while.16 = (s32[]{:T(128)}, f32[2048]{0:T(1024)S(1)}, f32[2048,512]{1,0:T(8,128)}, f32[2048]{0:T(1024)S(1)}, bf16[64,4096]{1,0:T(8,128)(2,1)}, /*index=5*/bf16[...) while((s32[]{:T(128)}, f32[2048]{0:T(1024)S(1)}, ...), condition=%wide.region_3.0_spmd.clone, body=%wide.region_1.0_spmd.clone.sunk | while | flops 2434993152 | bytes 39381208 | solution.py:57
  8.3 0.9 multiply_reduce_fusion.4
  9.3 5.0 %fusion.28 = bf16[2048,1024]{0,1:T(8,128)(2,1)} fusion(bf16[64,2048]{1,0:T(8,128)(2,1)} %get-tuple-element.267, f32[1024]{0:T(1024)S(1)} %multiply_reduce_fusion.4, f32[2048]{0:T(1024)S(1)} %get-tuple-element.265, bf16[64,4096]{1,0:T(8,128)(2,1)} %get-tuple-element.266, s32[]{:T(128)S(6)} %select_n.11), kind=kOutput, calls=%fused_computation.4.clone.1 | convolution fusion | flops 281018368 | bytes 4599812 | tf_op jit(solution)/shard_map/while/body/eval_jaxpr/dot_general | solution.py:46
  14.3 7.0 %select_add_fusion.5 = f32[2048,512]{1,0:T(8,128)} fusion(f32[2048,512]{1,0:T(8,128)} %get-tuple-element.252, bf16[2048,1024]{0,1:T(8,128)(2,1)} %fusion.28, pred[]{:T(512)S(6)} %compare.3, bf16[4096,512]{1,0:T(8,128)(2,1)} %get-tuple-element.269, s32[]{:T(128)S(6)} %select_n.11), kind=kOutput, calls=%fused_computation.5.clone.1 | convolution fusion | flops 2149580800 | bytes 13631493 | tf_op jit(solution)/shard_map/while/body/eval_jaxpr/dot_general | solution.py:53
  21.3 0.7 dynamic_slice.36
  22.6 0.9 multiply_reduce_fusion.4
  23.6 5.0 %fusion.28 = bf16[2048,1024]{0,1:T(8,128)(2,1)} fusion(bf16[64,2048]{1,0:T(8,128)(2,1)} %get-tuple-element.267, f32[1024]{0:T(1024)S(1)} %multiply_reduce_fusion.4, f32[2048]{0:T(1024)S(1)} %get-tuple-element.265, bf16[64,4096]{1,0:T(8,128)(2,1)} %get-tuple-element.266, s32[]{:T(128)S(6)} %select_n.11), kind=kOutput, calls=%fused_computation.4.clone.1 | convolution fusion | flops 281018368 | bytes 4599812 | tf_op jit(solution)/shard_map/while/body/eval_jaxpr/dot_general | solution.py:46
  28.6 8.3 %select_add_fusion.5 = f32[2048,512]{1,0:T(8,128)} fusion(f32[2048,512]{1,0:T(8,128)} %get-tuple-element.252, bf16[2048,1024]{0,1:T(8,128)(2,1)} %fusion.28, pred[]{:T(512)S(6)} %compare.3, bf16[4096,512]{1,0:T(8,128)(2,1)} %get-tuple-element.269, s32[]{:T(128)S(6)} %select_n.11), kind=kOutput, calls=%fused_computation.5.clone.1 | convolution fusion | flops 2149580800 | bytes 13631493 | tf_op jit(solution)/shard_map/while/body/eval_jaxpr/dot_general | solution.py:53
  36.8 0.7 dynamic_slice.36
  38.2 0.9 multiply_reduce_fusion.4
  39.1 5.0 %fusion.28 = bf16[2048,1024]{0,1:T(8,128)(2,1)} fusion(bf16[64,2048]{1,0:T(8,128)(2,1)} %get-tuple-element.267, f32[1024]{0:T(1024)S(1)} %multiply_reduce_fusion.4, f32[2048]{0:T(1024)S(1)} %get-tuple-element.265, bf16[64,4096]{1,0:T(8,128)(2,1)} %get-tuple-element.266, s32[]{:T(128)S(6)} %select_n.11), kind=kOutput, calls=%fused_computation.4.clone.1 | convolution fusion | flops 281018368 | bytes 4599812 | tf_op jit(solution)/shard_map/while/body/eval_jaxpr/dot_general | solution.py:46
  44.1 8.3 %select_add_fusion.5 = f32[2048,512]{1,0:T(8,128)} fusion(f32[2048,512]{1,0:T(8,128)} %get-tuple-element.252, bf16[2048,1024]{0,1:T(8,128)(2,1)} %fusion.28, pred[]{:T(512)S(6)} %compare.3, bf16[4096,512]{1,0:T(8,128)(2,1)} %get-tuple-element.269, s32[]{:T(128)S(6)} %select_n.11), kind=kOutput, calls=%fused_computation.5.clone.1 | convolution fusion | flops 2149580800 | bytes 13631493 | tf_op jit(solution)/shard_map/while/body/eval_jaxpr/dot_general | solution.py:53
  52.4 0.7 dynamic_slice.36
  53.8 0.9 multiply_reduce_fusion.4
  54.7 5.0 %fusion.28 = bf16[2048,1024]{0,1:T(8,128)(2,1)} fusion(bf16[64,2048]{1,0:T(8,128)(2,1)} %get-tuple-element.267, f32[1024]{0:T(1024)S(1)} %multiply_reduce_fusion.4, f32[2048]{0:T(1024)S(1)} %get-tuple-element.265, bf16[64,4096]{1,0:T(8,128)(2,1)} %get-tuple-element.266, s32[]{:T(128)S(6)} %select_n.11), kind=kOutput, calls=%fused_computation.4.clone.1 | convolution fusion | flops 281018368 | bytes 4599812 | tf_op jit(solution)/shard_map/while/body/eval_jaxpr/dot_general | solution.py:46
  59.7 8.3 %select_add_fusion.5 = f32[2048,512]{1,0:T(8,128)} fusion(f32[2048,512]{1,0:T(8,128)} %get-tuple-element.252, bf16[2048,1024]{0,1:T(8,128)(2,1)} %fusion.28, pred[]{:T(512)S(6)} %compare.3, bf16[4096,512]{1,0:T(8,128)(2,1)} %get-tuple-element.269, s32[]{:T(128)S(6)} %select_n.11), kind=kOutput, calls=%fused_computation.5.clone.1 | convolution fusion | flops 2149580800 | bytes 13631493 | tf_op jit(solution)/shard_map/while/body/eval_jaxpr/dot_general | solution.py:53
  68.0 0.7 dynamic_slice.36
  69.5 74.6 %reduce-scatter.3.cloned.1.call-done = f32[256,512]{1,0:T(8,128)} async-done(((f32[2048,512]{1,0:T(8,128)}), f32[256,512]{1,0:T(8,128)}) %reduce-scatter.3.cloned.1.call-update) | async-done | bytes 524304 | tf_op jit(solution)/shard_map/reduce_scatter | solution.py:15
  146.0 15.8 %all-reduce = f32[2048]{0:T(1024)S(1)} all-reduce(f32[2048]{0:T(1024)S(1)} %get-tuple-element.142), channel_id=2, replica_groups=mesh['grp'=2,'trn_0'=8,'trn_1'=8,'tst'=2] {'trn_0'}, use_global_device_ids=true, to_apply=%region_4.0.clone | all-reduce | flops 2048 | bytes 16384
  162.5 15.7 %all-reduce.1 = f32[256]{0:T(256)S(1)} all-reduce(f32[256]{0:T(256)S(1)} %dynamic-slice.1), channel_id=3, replica_groups=mesh['grp'=2,'trn_0'=8,'trn_1'=8,'tst'=2] {'trn_1'}, use_global_device_ids=true, to_apply=%region_5.0.clone | all-reduce | flops 256 | bytes 2048
  178.3 5.4 %reduce-scatter.5.cloned.1.call-done = f32[32,512]{1,0:T(8,128)} async-done(((f32[256,512]{1,0:T(8,128)}), f32[32,512]{1,0:T(8,128)}) %reduce-scatter.5.cloned.1.call-update) | async-done | bytes 65552 | tf_op jit(solution)/shard_map/reduce_scatter | solution.py:15
  183.7 1.0 multiply_reduce_fusion.2
  184.7 49.1 %all-gather = f32[64,32,2]{1,2,0:T(2,128)S(1)} all-gather(f32[1,32,2]{1,2,0:T(2,128)S(1)} %maximum_bitcast_fusion), channel_id=1, replica_groups=mesh['grp'=2,'trn_0'=8,'trn_1'=8,'tst'=2] {'trn_0','trn_1'}, dimensions={0}, use_global_device_ids=true | all-gather | bytes 16640 | tf_op jit(solution)/shard_map/all_gather | solution.py:22
  (39 shorter events, 5.0 us)
Async XLA Ops:
  7.2 136.9 %reduce-scatter.3.cloned.1.call-start = ((), (), s32[]{:S(2)}) async-start(), calls=%async_computation.2 | async-start | bytes 4718592 | tf_op jit(solution)/shard_map/reduce_scatter | solution.py:15
  14.3 7.7 %copy-start = (bf16[2048,1024]{0,1:T(8,128)(2,1)S(1)}, bf16[2048,1024]{0,1:T(8,128)(2,1)}, u32[]{:S(2)}) copy-start(bf16[2048,1024]{0,1:T(8,128)(2,1)} %fusion.28) | copy-start | bytes 12582916 | tf_op jit(solution)/shard_map/while
  28.6 9.0 %copy-start = (bf16[2048,1024]{0,1:T(8,128)(2,1)S(1)}, bf16[2048,1024]{0,1:T(8,128)(2,1)}, u32[]{:S(2)}) copy-start(bf16[2048,1024]{0,1:T(8,128)(2,1)} %fusion.28) | copy-start | bytes 12582916 | tf_op jit(solution)/shard_map/while
  44.1 9.0 %copy-start = (bf16[2048,1024]{0,1:T(8,128)(2,1)S(1)}, bf16[2048,1024]{0,1:T(8,128)(2,1)}, u32[]{:S(2)}) copy-start(bf16[2048,1024]{0,1:T(8,128)(2,1)} %fusion.28) | copy-start | bytes 12582916 | tf_op jit(solution)/shard_map/while
  59.7 9.0 %copy-start = (bf16[2048,1024]{0,1:T(8,128)(2,1)S(1)}, bf16[2048,1024]{0,1:T(8,128)(2,1)}, u32[]{:S(2)}) copy-start(bf16[2048,1024]{0,1:T(8,128)(2,1)} %fusion.28) | copy-start | bytes 12582916 | tf_op jit(solution)/shard_map/while
  69.3 74.8 %copy-start.2 = (u32[256]{0:T(256)S(1)}, u32[256]{0:T(256)}, u32[]{:S(2)}) copy-start(u32[256]{0:T(256)} %constant.56) | copy-start | bytes 3076
  69.4 76.1 %copy-start.1 = (u32[256]{0:T(256)S(1)}, u32[256]{0:T(256)}, u32[]{:S(2)}) copy-start(u32[256]{0:T(256)} %constant.60) | copy-start | bytes 3076
  69.4 114.3 %reduce-scatter.5.cloned.1.call-start = ((), (), s32[]{:S(2)}) async-start(), calls=%async_computation.3 | async-start | bytes 589824 | tf_op jit(solution)/shard_map/reduce_scatter | solution.py:15
Sparse Core Ops, SparseCore 0:
  69.5 74.5 reduce-scatter.2
  146.7 37.0 reduce-scatter.4
where the time goes:
time: 242 us; the launch traced here: 241 us
  blocking collectives  80.6 us (33%)
  waiting for transfers between devices  80.1 us (33%)
  matrix products  54.4 us (22%)
  between operations  15.4 us (6%)
  other arithmetic  5.82 us (2%)
  local copies, waits for them, and re-layouts  4.83 us (2%)
    reduce_scatter x2, waiting for transfers between devices, scatter_axes(): nearer = lax.psum_scatter(shard, axes[0], scatter_dimension=dim, tiled=True)  80 us
    all_gather x1, blocking collectives, turned_gather(): result, at, outs = (lax.all_gather(both, axis, axis=0, tiled=True), 0, [])  49.1 us
    dot_general x4, matrix products, step(): jnp.dot(kernel, fblock, preferred_element_type=jnp.float32)  31.8 us
    unnamed x2, blocking collectives  31.5 us
    dot_general x4, matrix products, step(): lax.dot_general(test_points, points, (((0,), (0,)), ((), ())), preferred_...  20 us
  transfers between devices with their start and end apart: 2, of which 2 were waited for; matrix products, arithmetic and copies ran while one was open for 1% of the time, Pallas kernels for 0%

commit v1 on v0

--- a/solution.py
+++ b/solution.py
@@ -19,7 +19,19 @@
 def turned_gather(arrays, axis, dims):
     turned = [jnp.moveaxis(a, dim, 0) for a, dim in zip(arrays, dims)]
     both = jnp.concatenate([t.reshape(len(t), -1) for t in turned], axis=1)
-    result, at, outs = (lax.all_gather(both, axis, axis=0, tiled=True), 0, [])
+    result, at, outs = (
+        jnp.concatenate(
+            jax.lax.all_to_all(
+                jnp.stack([both] * jax.lax.axis_size(axis)),
+                axis_name=axis,
+                split_axis=0,
+                concat_axis=0,
+            ),
+            0,
+        ),
+        0,
+        [],
+    )
     for t, dim in zip(turned, dims):
         piece = result[:, at : at + t[0].size].reshape(-1, *t.shape[1:])
         outs.append(jnp.moveaxis(piece, 0, dim))

time: 242 us -> 216 us (0.89)
  blocking collectives: 80.6 us -> 54.2 us
    all_gather x1 -> x0, blocking collectives: 49.1 us -> none  [turned_gather(): result, at, outs = (lax.all_gather(both, axis, axis=0, tiled=True), 0, [])]
    all_to_all x0 -> x1, blocking collectives: none -> 22.8 us  [turned_gather(): jax.lax.all_to_all(jnp.stack([both] * jax.lax.axis_size(axis)), axis_name...]
where the time goes in v1:
time: 216 us; the launch traced here: 215 us
  waiting for transfers between devices  80.1 us (37%)
  matrix products  54.4 us (25%)
  blocking collectives  54.2 us (25%)
  between operations  15.4 us (7%)
  other arithmetic  5.82 us (3%)
  local copies, waits for them, and re-layouts  4.85 us (2%)
    reduce_scatter x2, waiting for transfers between devices, scatter_axes(): nearer = lax.psum_scatter(shard, axes[0], scatter_dimension=dim, tiled=True)  80 us
    dot_general x4, matrix products, step(): jnp.dot(kernel, fblock, preferred_element_type=jnp.float32)  31.8 us
    unnamed x2, blocking collectives  31.5 us
    all_to_all x1, blocking collectives, turned_gather(): jax.lax.all_to_all(jnp.stack([both] * jax.lax.axis_size(axis)), axis_name...  22.8 us
    dot_general x4, matrix products, step(): lax.dot_general(test_points, points, (((0,), (0,)), ((), ())), preferred_...  20 us
  transfers between devices with their start and end apart: 2, of which 2 were waited for; matrix products, arithmetic and copies ran while one was open for 1% of the time, Pallas kernels for 0%

profile of v1, /device:TPU:514, one launch (start us, length us, event | category | flops | bytes accessed | tf_op | source)
XLA Modules:
  0.0 215.0 jit_solution(6810002341641825721)
XLA Ops:
  7.3 1.0 multiply_reduce_fusion.1
  8.3 61.1 %while.16 = (s32[]{:T(128)}, f32[2048]{0:T(1024)S(1)}, f32[2048,512]{1,0:T(8,128)}, f32[2048]{0:T(1024)S(1)}, bf16[64,4096]{1,0:T(8,128)(2,1)}, /*index=5*/bf16[...) while((s32[]{:T(128)}, f32[2048]{0:T(1024)S(1)}, ...), condition=%wide.region_3.0_spmd.clone, body=%wide.region_1.0_spmd.clone.sunk | while | flops 2434993152 | bytes 39381208 | solution.py:69
  8.3 0.9 multiply_reduce_fusion.4
  9.3 5.0 %fusion.28 = bf16[2048,1024]{0,1:T(8,128)(2,1)} fusion(bf16[64,2048]{1,0:T(8,128)(2,1)} %get-tuple-element.267, f32[1024]{0:T(1024)S(1)} %multiply_reduce_fusion.4, f32[2048]{0:T(1024)S(1)} %get-tuple-element.265, bf16[64,4096]{1,0:T(8,128)(2,1)} %get-tuple-element.266, s32[]{:T(128)S(6)} %select_n.11), kind=kOutput, calls=%fused_computation.4.clone.1 | convolution fusion | flops 281018368 | bytes 4599812 | tf_op jit(solution)/shard_map/while/body/eval_jaxpr/dot_general | solution.py:58
  14.3 7.0 %select_add_fusion.5 = f32[2048,512]{1,0:T(8,128)} fusion(f32[2048,512]{1,0:T(8,128)} %get-tuple-element.252, bf16[2048,1024]{0,1:T(8,128)(2,1)} %fusion.28, pred[]{:T(512)S(6)} %compare.3, bf16[4096,512]{1,0:T(8,128)(2,1)} %get-tuple-element.269, s32[]{:T(128)S(6)} %select_n.11), kind=kOutput, calls=%fused_computation.5.clone.1 | convolution fusion | flops 2149580800 | bytes 13631493 | tf_op jit(solution)/shard_map/while/body/eval_jaxpr/dot_general | solution.py:65
  21.3 0.7 dynamic_slice.36
  22.6 0.9 multiply_reduce_fusion.4
  23.6 5.0 %fusion.28 = bf16[2048,1024]{0,1:T(8,128)(2,1)} fusion(bf16[64,2048]{1,0:T(8,128)(2,1)} %get-tuple-element.267, f32[1024]{0:T(1024)S(1)} %multiply_reduce_fusion.4, f32[2048]{0:T(1024)S(1)} %get-tuple-element.265, bf16[64,4096]{1,0:T(8,128)(2,1)} %get-tuple-element.266, s32[]{:T(128)S(6)} %select_n.11), kind=kOutput, calls=%fused_computation.4.clone.1 | convolution fusion | flops 281018368 | bytes 4599812 | tf_op jit(solution)/shard_map/while/body/eval_jaxpr/dot_general | solution.py:58
  28.6 8.3 %select_add_fusion.5 = f32[2048,512]{1,0:T(8,128)} fusion(f32[2048,512]{1,0:T(8,128)} %get-tuple-element.252, bf16[2048,1024]{0,1:T(8,128)(2,1)} %fusion.28, pred[]{:T(512)S(6)} %compare.3, bf16[4096,512]{1,0:T(8,128)(2,1)} %get-tuple-element.269, s32[]{:T(128)S(6)} %select_n.11), kind=kOutput, calls=%fused_computation.5.clone.1 | convolution fusion | flops 2149580800 | bytes 13631493 | tf_op jit(solution)/shard_map/while/body/eval_jaxpr/dot_general | solution.py:65
  36.8 0.7 dynamic_slice.36
  38.2 0.9 multiply_reduce_fusion.4
  39.1 5.0 %fusion.28 = bf16[2048,1024]{0,1:T(8,128)(2,1)} fusion(bf16[64,2048]{1,0:T(8,128)(2,1)} %get-tuple-element.267, f32[1024]{0:T(1024)S(1)} %multiply_reduce_fusion.4, f32[2048]{0:T(1024)S(1)} %get-tuple-element.265, bf16[64,4096]{1,0:T(8,128)(2,1)} %get-tuple-element.266, s32[]{:T(128)S(6)} %select_n.11), kind=kOutput, calls=%fused_computation.4.clone.1 | convolution fusion | flops 281018368 | bytes 4599812 | tf_op jit(solution)/shard_map/while/body/eval_jaxpr/dot_general | solution.py:58
  44.1 8.3 %select_add_fusion.5 = f32[2048,512]{1,0:T(8,128)} fusion(f32[2048,512]{1,0:T(8,128)} %get-tuple-element.252, bf16[2048,1024]{0,1:T(8,128)(2,1)} %fusion.28, pred[]{:T(512)S(6)} %compare.3, bf16[4096,512]{1,0:T(8,128)(2,1)} %get-tuple-element.269, s32[]{:T(128)S(6)} %select_n.11), kind=kOutput, calls=%fused_computation.5.clone.1 | convolution fusion | flops 2149580800 | bytes 13631493 | tf_op jit(solution)/shard_map/while/body/eval_jaxpr/dot_general | solution.py:65
  52.4 0.7 dynamic_slice.36
  53.8 0.9 multiply_reduce_fusion.4
  54.7 5.0 %fusion.28 = bf16[2048,1024]{0,1:T(8,128)(2,1)} fusion(bf16[64,2048]{1,0:T(8,128)(2,1)} %get-tuple-element.267, f32[1024]{0:T(1024)S(1)} %multiply_reduce_fusion.4, f32[2048]{0:T(1024)S(1)} %get-tuple-element.265, bf16[64,4096]{1,0:T(8,128)(2,1)} %get-tuple-element.266, s32[]{:T(128)S(6)} %select_n.11), kind=kOutput, calls=%fused_computation.4.clone.1 | convolution fusion | flops 281018368 | bytes 4599812 | tf_op jit(solution)/shard_map/while/body/eval_jaxpr/dot_general | solution.py:58
  59.7 8.3 %select_add_fusion.5 = f32[2048,512]{1,0:T(8,128)} fusion(f32[2048,512]{1,0:T(8,128)} %get-tuple-element.252, bf16[2048,1024]{0,1:T(8,128)(2,1)} %fusion.28, pred[]{:T(512)S(6)} %compare.3, bf16[4096,512]{1,0:T(8,128)(2,1)} %get-tuple-element.269, s32[]{:T(128)S(6)} %select_n.11), kind=kOutput, calls=%fused_computation.5.clone.1 | convolution fusion | flops 2149580800 | bytes 13631493 | tf_op jit(solution)/shard_map/while/body/eval_jaxpr/dot_general | solution.py:65
  68.0 0.7 dynamic_slice.36
  69.5 74.6 %reduce-scatter.3.cloned.1.call-done = f32[256,512]{1,0:T(8,128)} async-done(((f32[2048,512]{1,0:T(8,128)}), f32[256,512]{1,0:T(8,128)}) %reduce-scatter.3.cloned.1.call-update) | async-done | bytes 524304 | tf_op jit(solution)/shard_map/reduce_scatter | solution.py:15
  146.0 15.8 %all-reduce = f32[2048]{0:T(1024)S(1)} all-reduce(f32[2048]{0:T(1024)S(1)} %get-tuple-element.142), channel_id=2, replica_groups=mesh['grp'=2,'trn_0'=8,'trn_1'=8,'tst'=2] {'trn_0'}, use_global_device_ids=true, to_apply=%region_4.0.clone | all-reduce | flops 2048 | bytes 16384
  162.5 15.7 %all-reduce.1 = f32[256]{0:T(256)S(1)} all-reduce(f32[256]{0:T(256)S(1)} %dynamic-slice.1), channel_id=3, replica_groups=mesh['grp'=2,'trn_0'=8,'trn_1'=8,'tst'=2] {'trn_1'}, use_global_device_ids=true, to_apply=%region_5.0.clone | all-reduce | flops 256 | bytes 2048
  178.3 5.4 %reduce-scatter.5.cloned.1.call-done = f32[32,512]{1,0:T(8,128)} async-done(((f32[256,512]{1,0:T(8,128)}), f32[32,512]{1,0:T(8,128)}) %reduce-scatter.5.cloned.1.call-update) | async-done | bytes 65552 | tf_op jit(solution)/shard_map/reduce_scatter | solution.py:15
  183.7 1.0 multiply_reduce_fusion.2
  184.7 22.8 %all_to_all.5 = f32[64,32,2]{1,2,0:T(2,128)S(1)} all-to-all(f32[64,32,2]{1,2,0:T(2,128)S(1)} %stack.2), channel_id=1, replica_groups=mesh['grp'=2,'trn_0'=8,'trn_1'=8,'tst'=2] {'trn_0','trn_1'}, dimensions={0} | all-to-all | bytes 32768 | tf_op jit(solution)/shard_map/all_to_all | solution.py:24
  (40 shorter events, 5.0 us)
Async XLA Ops:
  7.2 136.9 %reduce-scatter.3.cloned.1.call-start = ((), (), s32[]{:S(2)}) async-start(), calls=%async_computation.3 | async-start | bytes 4718592 | tf_op jit(solution)/shard_map/reduce_scatter | solution.py:15
  14.3 7.7 %copy-start = (bf16[2048,1024]{0,1:T(8,128)(2,1)S(1)}, bf16[2048,1024]{0,1:T(8,128)(2,1)}, u32[]{:S(2)}) copy-start(bf16[2048,1024]{0,1:T(8,128)(2,1)} %fusion.28) | copy-start | bytes 12582916 | tf_op jit(solution)/shard_map/while
  28.6 9.0 %copy-start = (bf16[2048,1024]{0,1:T(8,128)(2,1)S(1)}, bf16[2048,1024]{0,1:T(8,128)(2,1)}, u32[]{:S(2)}) copy-start(bf16[2048,1024]{0,1:T(8,128)(2,1)} %fusion.28) | copy-start | bytes 12582916 | tf_op jit(solution)/shard_map/while
  44.1 9.0 %copy-start = (bf16[2048,1024]{0,1:T(8,128)(2,1)S(1)}, bf16[2048,1024]{0,1:T(8,128)(2,1)}, u32[]{:S(2)}) copy-start(bf16[2048,1024]{0,1:T(8,128)(2,1)} %fusion.28) | copy-start | bytes 12582916 | tf_op jit(solution)/shard_map/while
  59.7 9.0 %copy-start = (bf16[2048,1024]{0,1:T(8,128)(2,1)S(1)}, bf16[2048,1024]{0,1:T(8,128)(2,1)}, u32[]{:S(2)}) copy-start(bf16[2048,1024]{0,1:T(8,128)(2,1)} %fusion.28) | copy-start | bytes 12582916 | tf_op jit(solution)/shard_map/while
  69.3 74.8 %copy-start.2 = (u32[256]{0:T(256)S(1)}, u32[256]{0:T(256)}, u32[]{:S(2)}) copy-start(u32[256]{0:T(256)} %constant.56) | copy-start | bytes 3076
  69.4 76.1 %copy-start.1 = (u32[256]{0:T(256)S(1)}, u32[256]{0:T(256)}, u32[]{:S(2)}) copy-start(u32[256]{0:T(256)} %constant.60) | copy-start | bytes 3076
  69.4 114.3 %reduce-scatter.5.cloned.1.call-start = ((), (), s32[]{:S(2)}) async-start(), calls=%async_computation.4 | async-start | bytes 589824 | tf_op jit(solution)/shard_map/reduce_scatter | solution.py:15
Sparse Core Ops, SparseCore 0:
  69.5 74.5 reduce-scatter.2
  146.7 37.0 reduce-scatter.4
